TPU v7x, 32 devices: a whole 2x2x4 slice. The times are simulated.
32 devices in a mesh: dp: 8 (over y, x, core), tensor: 4 (over z).
Axes of the slice: x: 2, y: 2, z: 4, core: 2. Of those that a mesh axis runs over, the one named last changes fastest.
Arguments:
- tokens: bfloat16 [12288, 2048], P(('dp', 'tensor')), may hold values from -6 to 6
- segments: int32 [12288], P('dp'), may hold values from 0 to 4, as said below
- cotangent: bfloat16 [12288, 2048], P(('dp', 'tensor')), may hold values from -6 to 6
- ln1_gain: bfloat16 [2048], replicated, may hold values from 0.5 to 1.5
- ln1_shift: bfloat16 [2048], replicated, may hold values from -1.5 to 1.5
- w_query: bfloat16 [2048, 2048], P('dp', 'tensor'), may hold values from -0.1875 to 0.1875
- b_query: bfloat16 [2048], P('tensor'), may hold values from -1.5 to 1.5
- w_key: bfloat16 [2048, 2048], P('dp', 'tensor'), may hold values from -0.1875 to 0.1875
- w_value: bfloat16 [2048, 2048], P('dp', 'tensor'), may hold values from -0.125 to 0.125
- b_value: bfloat16 [2048], P('tensor'), may hold values from -1.5 to 1.5
- w_out: bfloat16 [2048, 2048], P('tensor', 'dp'), may hold values from -0.5 to 0.5
- b_out: bfloat16 [2048], replicated, may hold values from -1.5 to 1.5
- ln2_gain: bfloat16 [2048], replicated, may hold values from 0.5 to 1.5
- ln2_shift: bfloat16 [2048], replicated, may hold values from -1.5 to 1.5
- w_up: bfloat16 [2048, 8192], P('dp', 'tensor'), may hold values from -0.125 to 0.125
- b_up: bfloat16 [8192], P('tensor'), may hold values from -1.5 to 1.5
- w_down: bfloat16 [8192, 2048], P('tensor', 'dp'), may hold values from -0.0625 to 0.0625
- b_down: bfloat16 [2048], replicated, may hold values from -1.5 to 1.5
Outputs:
- output: bfloat16 [12288, 2048], P(('dp', 'tensor'))
- input_grad: bfloat16 [12288, 2048], P(('dp', 'tensor'))
- grad_ln1_gain: float32 [2048], replicated
- grad_ln1_shift: float32 [2048], replicated
- grad_w_query: float32 [2048, 2048], P('dp', 'tensor')
- grad_b_query: float32 [2048], P('tensor')
- grad_w_key: float32 [2048, 2048], P('dp', 'tensor')
- grad_w_value: float32 [2048, 2048], P('dp', 'tensor')
- grad_b_value: float32 [2048], P('tensor')
- grad_w_out: float32 [2048, 2048], P('tensor', 'dp')
- grad_b_out: float32 [2048], replicated
- grad_ln2_gain: float32 [2048], replicated
- grad_ln2_shift: float32 [2048], replicated
- grad_w_up: float32 [2048, 8192], P('dp', 'tensor')
- grad_b_up: float32 [8192], P('tensor')
- grad_w_down: float32 [8192, 2048], P('tensor', 'dp')
- grad_b_down: float32 [2048], replicated
Inputs may be any that keep to these rules, and one draw needn't show every extreme that they name: Within each group of 1536 tokens the first 1024 have segment 0; the rest form 4 contiguous runs with segments 1 to 4 in rising order, each run 128 // 2 to 192 tokens long; in every group one run is exactly 192 long.
All inputs are finite; a program needn't handle non-finite values.
Results may differ from a plain program's by a relative error of at most 0.017.
Values may be sent and summed in bfloat16 or wider, within the bound.
A program may use at most 320 MiB of HBM per device.

v0:
```python
import math
import jax
import jax.numpy as jnp
from jax import lax
from jax.sharding import PartitionSpec as P

HDIM = 128
QBLK = 768
EPS = 1e-05
NEG = -1e30


def layer_norm(values, norm_gain, norm_shift):
    row_mean = jnp.mean(values, axis=-1, keepdims=True)
    centred = values - row_mean
    row_var = jnp.mean(centred * centred, axis=-1, keepdims=True)
    return centred * lax.rsqrt(row_var + EPS) * norm_gain + norm_shift


def gelu_exact(values):
    return jax.nn.gelu(values, approximate=False)


def row_dot(left_side, right_side):
    return jnp.dot(left_side, right_side, preferred_element_type=jnp.float32)


def left_dot(left_side, right_side):
    return lax.dot_general(
        left_side, right_side, (((0,), (0,)), ((), ())), preferred_element_type=jnp.float32
    )


def back_dot(left_side, right_side):
    return lax.dot_general(
        left_side, right_side, (((1,), (1,)), ((), ())), preferred_element_type=jnp.float32
    )


def visible(segments, first_row, row_count, key_end):
    query_pos = first_row + jnp.arange(row_count)
    key_pos = jnp.arange(key_end)
    seg_query = segments[first_row : first_row + row_count]
    seg_key = segments[:key_end]
    causal = key_pos[None, :] <= query_pos[:, None]
    shared = (seg_key[None, :] == seg_query[:, None]) | (seg_key[None, :] == 0)
    return causal & shared


def attend_block(queries, key_rows, value_rows, allowed):
    scores = jnp.einsum("qhd,khd->hqk", queries, key_rows, preferred_element_type=jnp.float32)
    scores = jnp.where(allowed[None], scores, NEG)
    row_top = jnp.max(scores, axis=-1, keepdims=True)
    raised = jnp.exp(scores - row_top)
    row_total = jnp.sum(raised, axis=-1, keepdims=True)
    weights = raised / row_total
    mixed = jnp.einsum(
        "hqk,khd->qhd", weights.astype(jnp.bfloat16), value_rows, preferred_element_type=jnp.float32
    )
    return (mixed.astype(jnp.bfloat16), row_top + jnp.log(row_total))


def attend_back(queries, key_rows, value_rows, grad_out, log_total, allowed):
    scores = jnp.einsum("qhd,khd->hqk", queries, key_rows, preferred_element_type=jnp.float32)
    weights = jnp.where(allowed[None], jnp.exp(scores - log_total), 0.0)
    grad_weights = jnp.einsum(
        "qhd,khd->hqk", grad_out, value_rows, preferred_element_type=jnp.float32
    )
    inner = jnp.sum(weights * grad_weights, axis=-1, keepdims=True)
    grad_scores = (weights * (grad_weights - inner)).astype(jnp.bfloat16)
    grad_query = jnp.einsum(
        "hqk,khd->qhd", grad_scores, key_rows, preferred_element_type=jnp.float32
    )
    grad_key = jnp.einsum("hqk,qhd->khd", grad_scores, queries, preferred_element_type=jnp.float32)
    grad_value = jnp.einsum(
        "hqk,qhd->khd", weights.astype(jnp.bfloat16), grad_out, preferred_element_type=jnp.float32
    )
    return (grad_query, grad_key, grad_value)


def on_device(
    tokens,
    segments,
    cotangent,
    ln1_gain,
    ln1_shift,
    w_query,
    b_query,
    w_key,
    w_value,
    b_value,
    w_out,
    b_out,
    ln2_gain,
    ln2_shift,
    w_up,
    b_up,
    w_down,
    b_down,
):
    score_scale = 1.0 / math.sqrt(HDIM)
    full_query, full_key, full_value, full_out, full_up, full_down = (
        lax.all_gather(w_query, "dp", axis=0, tiled=True),
        lax.all_gather(w_key, "dp", axis=0, tiled=True),
        lax.all_gather(w_value, "dp", axis=0, tiled=True),
        lax.all_gather(w_out, "dp", axis=1, tiled=True),
        lax.all_gather(w_up, "dp", axis=0, tiled=True),
        lax.all_gather(w_down, "dp", axis=1, tiled=True),
    )
    group_len = segments.shape[0]
    head_cols = full_query.shape[1]
    heads_here = head_cols // HDIM
    block_count = group_len // QBLK
    inputs = tokens.astype(jnp.float32)
    normed_one, norm_one_back = jax.vjp(
        layer_norm, inputs, ln1_gain.astype(jnp.float32), ln1_shift.astype(jnp.float32)
    )
    h_one = normed_one.astype(jnp.bfloat16)
    h_one_full = lax.all_gather(h_one, "tensor", axis=0, tiled=True)
    w_qkv = jnp.concatenate([full_query, full_key, full_value], axis=1)
    w_kv = w_qkv[:, head_cols:]
    projected = row_dot(h_one_full, w_qkv)
    queries = ((projected[:, :head_cols] + b_query.astype(jnp.float32)) * score_scale).astype(
        jnp.bfloat16
    )
    key_rows = projected[:, head_cols : 2 * head_cols].astype(jnp.bfloat16)
    value_rows = (projected[:, 2 * head_cols :] + b_value.astype(jnp.float32)).astype(jnp.bfloat16)
    query3 = queries.reshape(group_len, heads_here, HDIM)
    key3 = key_rows.reshape(group_len, heads_here, HDIM)
    value3 = value_rows.reshape(group_len, heads_here, HDIM)
    pieces = []
    totals = []
    for block in range(block_count):
        first_row = block * QBLK
        key_end = first_row + QBLK
        allowed = visible(segments, first_row, QBLK, key_end)
        mixed_block, log_total = attend_block(
            query3[first_row:key_end], key3[:key_end], value3[:key_end], allowed
        )
        pieces.append(mixed_block)
        totals.append(log_total)
    attended = jnp.concatenate(pieces, axis=0).reshape(group_len, head_cols)
    resid = (
        inputs
        + lax.psum_scatter(row_dot(attended, full_out), "tensor", scatter_dimension=0, tiled=True)
        + b_out.astype(jnp.float32)
    )
    normed_two, norm_two_back = jax.vjp(
        layer_norm, resid, ln2_gain.astype(jnp.float32), ln2_shift.astype(jnp.float32)
    )
    h_two = normed_two.astype(jnp.bfloat16)
    h_two_full = lax.all_gather(h_two, "tensor", axis=0, tiled=True)
    pre_act = row_dot(h_two_full, full_up) + b_up.astype(jnp.float32)
    activated, gelu_back = jax.vjp(gelu_exact, pre_act)
    act_low = activated.astype(jnp.bfloat16)
    output = (
        resid
        + lax.psum_scatter(
            row_dot(act_low, full_down).astype(jnp.bfloat16),
            "tensor",
            scatter_dimension=0,
            tiled=True,
        ).astype(jnp.float32)
        + b_down.astype(jnp.float32)
    ).astype(jnp.bfloat16)
    grad_y = cotangent.astype(jnp.float32)
    grad_y_full = lax.all_gather(cotangent, "tensor", axis=0, tiled=True)
    grad_down = left_dot(act_low, grad_y_full)
    grad_act = back_dot(grad_y_full, full_down)
    grad_pre = gelu_back(grad_act)[0].astype(jnp.bfloat16)
    grad_bias_up = jnp.sum(grad_pre.astype(jnp.float32), axis=0)
    grad_up = left_dot(h_two_full, grad_pre)
    grad_h_two = lax.psum_scatter(
        back_dot(grad_pre, full_up), "tensor", scatter_dimension=0, tiled=True
    )
    grad_resid_norm, grad_gain_two, grad_shift_two = norm_two_back(grad_h_two)
    grad_resid = grad_y + grad_resid_norm
    grad_mix = grad_resid.astype(jnp.bfloat16)
    grad_bias_out = jnp.sum(grad_mix.astype(jnp.float32), axis=0)
    grad_bias_down = jnp.sum(grad_y, axis=0)
    grad_mix_full = lax.all_gather(grad_mix, "tensor", axis=0, tiled=True)
    grad_out_w = left_dot(attended, grad_mix_full)
    grad_att = (
        back_dot(grad_mix_full, full_out).astype(jnp.bfloat16).reshape(group_len, heads_here, HDIM)
    )
    grad_key_sum = jnp.zeros((group_len, heads_here, HDIM), jnp.float32)
    grad_value_sum = jnp.zeros((group_len, heads_here, HDIM), jnp.float32)
    query_grads = []
    for block in range(block_count):
        first_row = block * QBLK
        key_end = first_row + QBLK
        allowed = visible(segments, first_row, QBLK, key_end)
        grad_q_block, grad_k_part, grad_v_part = attend_back(
            query3[first_row:key_end],
            key3[:key_end],
            value3[:key_end],
            grad_att[first_row:key_end],
            totals[block],
            allowed,
        )
        query_grads.append(grad_q_block.astype(jnp.bfloat16))
        grad_key_sum = grad_key_sum.at[:key_end].add(grad_k_part)
        grad_value_sum = grad_value_sum.at[:key_end].add(grad_v_part)
    grad_q = jnp.concatenate(query_grads, axis=0).reshape(group_len, head_cols)
    grad_k = grad_key_sum.reshape(group_len, head_cols).astype(jnp.bfloat16)
    grad_v = grad_value_sum.reshape(group_len, head_cols).astype(jnp.bfloat16)
    grad_qkv = jnp.concatenate([grad_q, grad_k, grad_v], axis=1)
    grad_qkv_w = left_dot(h_one_full, grad_qkv)
    grad_wq = grad_qkv_w[:, :head_cols] * score_scale
    grad_wk = grad_qkv_w[:, head_cols : 2 * head_cols]
    grad_wv = grad_qkv_w[:, 2 * head_cols :]
    grad_bias_query = jnp.sum(grad_q.astype(jnp.float32), axis=0) * score_scale
    grad_bias_value = jnp.sum(grad_v.astype(jnp.float32), axis=0)
    grad_h_one = lax.psum_scatter(
        (
            back_dot(grad_qkv[:, :head_cols], full_query) * score_scale
            + back_dot(grad_qkv[:, head_cols:], w_kv)
        ).astype(jnp.bfloat16),
        "tensor",
        scatter_dimension=0,
        tiled=True,
    ).astype(jnp.float32)
    grad_in_norm, grad_gain_one, grad_shift_one = norm_one_back(grad_h_one)
    input_grad = (grad_resid + grad_in_norm).astype(jnp.bfloat16)
    sent_query, sent_key, sent_value, sent_out, sent_up, sent_down = (
        lax.psum_scatter(
            grad_wq.astype(jnp.bfloat16), "dp", scatter_dimension=0, tiled=True
        ).astype(jnp.float32),
        lax.psum_scatter(
            grad_wk.astype(jnp.bfloat16), "dp", scatter_dimension=0, tiled=True
        ).astype(jnp.float32),
        lax.psum_scatter(
            grad_wv.astype(jnp.bfloat16), "dp", scatter_dimension=0, tiled=True
        ).astype(jnp.float32),
        lax.psum_scatter(
            grad_out_w.astype(jnp.bfloat16), "dp", scatter_dimension=1, tiled=True
        ).astype(jnp.float32),
        lax.psum_scatter(
            grad_up.astype(jnp.bfloat16), "dp", scatter_dimension=0, tiled=True
        ).astype(jnp.float32),
        lax.psum_scatter(
            grad_down.astype(jnp.bfloat16), "dp", scatter_dimension=1, tiled=True
        ).astype(jnp.float32),
    )
    summed_query, summed_value, summed_up = lax.psum(
        (grad_bias_query, grad_bias_value, grad_bias_up), "dp"
    )
    gain_one_sum, shift_one_sum, gain_two_sum, shift_two_sum, bias_out_sum, bias_down_sum = (
        lax.psum(
            (
                grad_gain_one,
                grad_shift_one,
                grad_gain_two,
                grad_shift_two,
                grad_bias_out,
                grad_bias_down,
            ),
            ("dp", "tensor"),
        )
    )
    return (
        output,
        input_grad,
        gain_one_sum,
        shift_one_sum,
        sent_query,
        summed_query,
        sent_key,
        sent_value,
        summed_value,
        sent_out,
        bias_out_sum,
        gain_two_sum,
        shift_two_sum,
        sent_up,
        summed_up,
        sent_down,
        bias_down_sum,
    )


def solution(mesh):
    return jax.shard_map(
        on_device,
        mesh=mesh,
        in_specs=(
            P(("dp", "tensor"), None),
            P("dp"),
            P(("dp", "tensor"), None),
            P(),
            P(),
            P("dp", "tensor"),
            P("tensor"),
            P("dp", "tensor"),
            P("dp", "tensor"),
            P("tensor"),
            P("tensor", "dp"),
            P(),
            P(),
            P(),
            P("dp", "tensor"),
            P("tensor"),
            P("tensor", "dp"),
            P(),
        ),
        out_specs=(
            P(("dp", "tensor"), None),
            P(("dp", "tensor"), None),
            P(),
            P(),
            P("dp", "tensor"),
            P("tensor"),
            P("dp", "tensor"),
            P("dp", "tensor"),
            P("tensor"),
            P("tensor", "dp"),
            P(),
            P(),
            P(),
            P("dp", "tensor"),
            P("tensor"),
            P("tensor", "dp"),
            P(),
        ),
        check_vma=False,
    )
```

profile of v0, /device:TPU:0, one launch (start us, length us, event | category | flops | bytes accessed | tf_op | source)
XLA Modules:
  0.0 1852.3 jit_solution(1122255741000545251)
XLA Ops:
  12.6 2.0 fusion.55
  17.6 2.2 fusion.36
  19.8 20.7 %all-gather.13.cloned.1.call-done = bf16[2048,512]{1,0:T(8,128)(2,1)} async-done(((bf16[256,512]{1,0:T(8,128)(2,1)}), bf16[2048,512]{1,0:T(8,128)(2,1)}) %all-gather.13.cloned.1.call-update) | async-done | bytes 2097168 | tf_op jit(solution)/shard_map/all_gather | solution.py:103
  40.5 29.7 %all-gather.15.cloned.1.call-done = bf16[2048,512]{1,0:T(8,128)(2,1)} async-done(((bf16[256,512]{1,0:T(8,128)(2,1)}), bf16[2048,512]{1,0:T(8,128)(2,1)}) %all-gather.15.cloned.1.call-update) | async-done | bytes 2097168 | tf_op jit(solution)/shard_map/all_gather | solution.py:104
  70.2 29.7 %all-gather.17.cloned.1.call-done = bf16[2048,512]{1,0:T(8,128)(2,1)} async-done(((bf16[256,512]{1,0:T(8,128)(2,1)}), bf16[2048,512]{1,0:T(8,128)(2,1)}) %all-gather.17.cloned.1.call-update) | async-done | bytes 2097168 | tf_op jit(solution)/shard_map/all_gather | solution.py:105
  99.9 117.4 %all-gather.11.cloned.1.call-done = bf16[1536,2048]{1,0:T(8,128)(2,1)} async-done(((bf16[384,2048]{1,0:T(8,128)(2,1)}), bf16[1536,2048]{1,0:T(8,128)(2,1)}) %all-gather.11.cloned.1.call-update) | async-done | bytes 6291472 | tf_op jit(solution)/shard_map/all_gather | solution.py:119
  217.2 17.0 fusion.99
  235.4 1.9 slice.182
  237.3 3.9 fusion.60
  247.8 3.8 fusion.80
  251.6 4.3 select_reduce_fusion
  255.8 5.1 fusion
  262.6 9.2 fusion.79
  272.0 8.5 fusion.101
  281.5 209.5 %reduce-scatter.11.cloned.1.call-done = f32[384,2048]{1,0:T(8,128)} async-done(((f32[1536,2048]{1,0:T(8,128)}), f32[384,2048]{1,0:T(8,128)}) %reduce-scatter.11.cloned.1.call-update) | async-done | bytes 3145744 | tf_op jit(solution)/shard_map/reduce_scatter | solution.py:145
  491.0 2.4 fusion.93
  498.7 49.4 %all-gather.23.cloned.1.call-done = bf16[2048,2048]{1,0:T(8,128)(2,1)} async-done(((bf16[256,2048]{1,0:T(8,128)(2,1)}), bf16[2048,2048]{1,0:T(8,128)(2,1)}) %all-gather.23.cloned.1.call-update) | async-done | bytes 8388624 | tf_op jit(solution)/shard_map/all_gather | solution.py:107
  548.2 117.5 %all-gather.21.cloned.1.call-done = bf16[1536,2048]{1,0:T(8,128)(2,1)} async-done(((bf16[384,2048]{1,0:T(8,128)(2,1)}), bf16[1536,2048]{1,0:T(8,128)(2,1)}) %all-gather.21.cloned.1.call-update) | async-done | bytes 6291472 | tf_op jit(solution)/shard_map/all_gather | solution.py:152
  665.7 19.1 %fusion.102 = f32[1536,2048]{1,0:T(8,128)} fusion(bf16[1536,2048]{1,0:T(8,128)(2,1)} %all-gather.21.cloned.1.call-done, bf16[2048,2048]{1,0:T(8,128)(2,1)} %all-gather.23.cloned.1.call-done), kind=kOutput, calls=%fused_computation.163 | convolution fusion | flops 12884901888 | bytes 27262976 | tf_op jit(solution)/shard_map/dot_general | solution.py:25
  684.8 96.0 %all-gather.27.cloned.1.call-done = bf16[1536,2048]{1,0:T(8,128)(2,1)} async-done(((bf16[384,2048]{1,0:T(8,128)(2,1)}), bf16[1536,2048]{1,0:T(8,128)(2,1)}) %all-gather.27.cloned.1.call-update) | async-done | bytes 6291472 | tf_op jit(solution)/shard_map/all_gather | solution.py:167
  780.8 55.8 %all-gather.25.cloned.1.call-done = bf16[2048,2048]{1,0:T(8,128)(2,1)} async-done(((bf16[2048,256]{1,0:T(8,128)(2,1)}), bf16[2048,2048]{1,0:T(8,128)(2,1)}) %all-gather.25.cloned.1.call-update) | async-done | bytes 8388624 | tf_op jit(solution)/shard_map/all_gather | solution.py:108
  836.6 48.6 %convert_reduce_fusion = (f32[2048]{0:T(1024)}, bf16[1536,2048]{1,0:T(8,128)(2,1)S(1)}, f32[1536,2048]{1,0:T(8,128)}) fusion(f32[1536,2048]{1,0:T(8,128)} %fusion.102, f32[2048]{0:T(1024)S(1)} %convert_element_type.195, bf16[1536,2048]{1,0:T(8,128)(2,1)} %all-gather.27.cloned.1.call-done, bf16[2048,2048]{1,0:T(8,128)(2,1)} %all-gather.25.cloned.1.call-done), kind=kOutput, calls=%fused_computation.9 | convolution fusion | flops 13120829440 | bytes 46153728 | tf_op jit(solution)/shard_map/dot_general | solution.py:35
  885.2 2.6 copy-done.78
  887.8 18.3 fusion.103
  906.1 10.7 multiply_convert_fusion.1
  916.9 2.7 copy-done.28
  919.6 17.5 convolution_convert_fusion.2
  937.8 180.3 %reduce-scatter.15.cloned.1.call-done = f32[384,2048]{1,0:T(8,128)} async-done(((f32[1536,2048]{1,0:T(8,128)}), f32[384,2048]{1,0:T(8,128)}) %reduce-scatter.15.cloned.1.call-update) | async-done | bytes 3145744 | tf_op jit(solution)/shard_map/reduce_scatter | solution.py:173
  1118.2 3.5 multiply_reduce_fusion.2
  1121.7 110.5 %reduce-scatter.13.cloned.1.call-done = bf16[384,2048]{1,0:T(8,128)(2,1)} async-done(((bf16[1536,2048]{1,0:T(8,128)(2,1)}), bf16[384,2048]{1,0:T(8,128)(2,1)}) %reduce-scatter.13.cloned.1.call-update) | async-done | bytes 1572880 | tf_op jit(solution)/shard_map/reduce_scatter | solution.py:158
  1232.2 4.8 fusion.92
  1238.6 2.3 convert_reduce_fusion.4
  1241.0 19.4 %convolution_convert_fusion = bf16[2048,2048]{1,0:T(8,128)(2,1)} fusion(bf16[1536,2048]{1,0:T(8,128)(2,1)} %copy-done.28, bf16[1536,2048]{1,0:T(8,128)(2,1)} %all-gather.27.cloned.1.call-done), kind=kOutput, calls=%fused_computation.39 | convolution fusion | flops 12889096192 | bytes 20971520 | tf_op jit(solution)/shard_map/dot_general | solution.py:29
  1260.6 19.3 %convolution_convert_fusion.1 = bf16[2048,2048]{1,0:T(8,128)(2,1)} fusion(bf16[1536,2048]{1,0:T(8,128)(2,1)} %all-gather.21.cloned.1.call-done, bf16[1536,2048]{1,0:T(8,128)(2,1)} %copy-done.78), kind=kOutput, calls=%fused_computation.40 | convolution fusion | flops 12889096192 | bytes 20971520 | tf_op jit(solution)/shard_map/dot_general | solution.py:29
  1280.7 76.2 %all-gather.29.cloned.1.call-done = bf16[1536,2048]{1,0:T(8,128)(2,1)} async-done(((bf16[384,2048]{1,0:T(8,128)(2,1)}), bf16[1536,2048]{1,0:T(8,128)(2,1)}) %all-gather.29.cloned.1.call-update) | async-done | bytes 6291472 | tf_op jit(solution)/shard_map/all_gather | solution.py:181
  1356.9 6.9 convolution_convert_fusion.4
  1364.7 9.7 multiply_reduce_fusion.1
  1374.4 10.9 multiply_convert_fusion.2
  1385.3 4.2 fusion.77
  1389.5 2.8 convolution_bitcast_fusion.1
  1392.3 17.0 multiply_reduce_fusion
  1409.3 14.8 multiply_convert_fusion
  1424.1 2.6 fusion.68
  1426.7 4.1 fusion.78
  1430.8 4.4 fusion.72
  1435.2 7.4 convolution_convert_fusion.3
  1442.6 14.6 convert_reduce_fusion.5
  1459.2 15.3 fusion.100
  1474.5 2.3 fusion.95
  1477.4 4.2 fusion.39
  1481.7 12.1 fusion.40
  1493.9 8.4 add_convert_fusion
  1502.3 2.7 convert_element_type.233
  1505.1 2.9 convert_element_type.230
  1508.3 24.5 %all-reduce.3 = (f32[512]{0:T(512)}, f32[512]{0:T(512)}, f32[2048]{0:T(1024)}) all-reduce(f32[512]{0:T(512)S(1)} %multiply_bitcast_fusion, f32[512]{0:T(512)S(1)} %bitcast.105, f32[2048]{0:T(1024)S(1)} %copy-done.69), channel_id=1, replica_groups=mesh['dp'=8,'tensor'=4] {'dp'}, use_global_device_ids=true, to_apply=%region_24.25 | all-reduce | flops 3072 | bytes 24576 | tf_op jit(solution)/shard_map/psum | solution.py:245
  1532.8 16.1 reduce-scatter.25.cloned.1.call-done
  1550.7 42.5 %reduce-scatter.21.cloned.1.call-done = bf16[256,512]{1,0:T(8,128)(2,1)} async-done(((bf16[2048,512]{1,0:T(8,128)(2,1)}), bf16[256,512]{1,0:T(8,128)(2,1)}) %reduce-scatter.21.cloned.1.call-update) | async-done | bytes 262160 | tf_op jit(solution)/shard_map/reduce_scatter | solution.py:229
  1595.0 42.5 %reduce-scatter.23.cloned.1.call-done = bf16[256,512]{1,0:T(8,128)(2,1)} async-done(((bf16[2048,512]{1,0:T(8,128)(2,1)}), bf16[256,512]{1,0:T(8,128)(2,1)}) %reduce-scatter.23.cloned.1.call-update) | async-done | bytes 262160 | tf_op jit(solution)/shard_map/reduce_scatter | solution.py:232
  1639.3 42.6 %reduce-scatter.19.cloned.1.call-done = bf16[256,512]{1,0:T(8,128)(2,1)} async-done(((bf16[2048,512]{1,0:T(8,128)(2,1)}), bf16[256,512]{1,0:T(8,128)(2,1)}) %reduce-scatter.19.cloned.1.call-update) | async-done | bytes 262160 | tf_op jit(solution)/shard_map/reduce_scatter | solution.py:226
  1683.7 111.2 %reduce-scatter.17.cloned.1.call-done = bf16[384,2048]{1,0:T(8,128)(2,1)} async-done(((bf16[1536,2048]{1,0:T(8,128)(2,1)}), bf16[384,2048]{1,0:T(8,128)(2,1)}) %reduce-scatter.17.cloned.1.call-update) | async-done | bytes 1572880 | tf_op jit(solution)/shard_map/reduce_scatter | solution.py:214
  1794.9 2.5 convert_reduce_fusion.1
  1797.4 2.9 fusion.58
  1800.4 2.8 convert_reduce_fusion.3
  1803.2 42.0 %all-reduce.2 = (f32[2048]{0:T(1024)}, f32[2048]{0:T(1024)}, f32[2048]{0:T(1024)}, f32[2048]{0:T(1024)}, f32[2048]{0:T(1024)}, /*index=5*/f32[2048]{0:T(1024)}) all-reduce(f32[2048]{0:T(1024)S(1)} %get-tuple-element.83, f32[2048]{0:T(1024)S(1)} %get-tuple-element.86, ...), channel_id=1, replica_groups=mesh['dp'=8,'tensor'=4] {'dp','tensor'}, use_global_device_ids=true, to_apply=%region_19.20 | all-reduce | flops 12288 | bytes 98304 | tf_op jit(solution)/shard_map/psum | solution.py:249
  (247 shorter events, 38.7 us)
Async XLA Ops:
  7.2 7.4 copy-start.4
  7.2 9.9 copy-start.47
  7.2 9.9 copy-start.75
  7.2 9.9 copy-start.76
  7.2 33.2 %all-gather.13.cloned.1.call-start = ((), (), s32[]{:S(2)}) async-start(), calls=%async_computation.11 | async-start | bytes 2359296 | tf_op jit(solution)/shard_map/all_gather | solution.py:103
  8.0 62.2 %all-gather.15.cloned.1.call-start = ((), (), s32[]{:S(2)}) async-start(), calls=%async_computation.12 | async-start | bytes 2359296 | tf_op jit(solution)/shard_map/all_gather | solution.py:104
  8.7 91.2 %all-gather.17.cloned.1.call-start = ((), (), s32[]{:S(2)}) async-start(), calls=%async_computation.13 | async-start | bytes 2359296 | tf_op jit(solution)/shard_map/all_gather | solution.py:105
  9.4 207.8 %all-gather.11.cloned.1.call-start = ((), (), s32[]{:S(2)}) async-start(), calls=%async_computation.10 | async-start | bytes 7864320 | tf_op jit(solution)/shard_map/all_gather | solution.py:119
  16.4 255.6 %all-gather.19.cloned.1.call-start = ((), (), s32[]{:S(2)}) async-start(), calls=%async_computation.14 | async-start | bytes 2359296 | tf_op jit(solution)/shard_map/all_gather | solution.py:106
  17.0 473.9 %reduce-scatter.11.cloned.1.call-start = ((), (), s32[]{:S(2)}) async-start(), calls=%async_computation.15 | async-start | bytes 15728640 | tf_op jit(solution)/shard_map/reduce_scatter | solution.py:145
  17.6 228.3 %copy-start.13 = (pred[768,768]{0,1:T(8,128)(4,1)}, pred[768,768]{0,1:T(8,128)(4,1)S(1)}, u32[]{:S(2)}) copy-start(pred[768,768]{0,1:T(8,128)(4,1)S(1)} %fusion.69) | copy-start | bytes 1769476
  19.8 242.5 %copy-start.6 = (pred[768,1536]{1,0:T(8,128)(4,1)}, pred[768,1536]{1,0:T(8,128)(4,1)S(1)}, u32[]{:S(2)}) copy-start(pred[768,1536]{1,0:T(8,128)(4,1)S(1)} %fusion.36) | copy-start | bytes 3538948
  235.4 7.0 copy-start.20
  237.3 14.3 copy-start.11
  241.2 21.1 %copy-start.15 = (bf16[1536,512]{0,1:T(8,128)(2,1)}, bf16[1536,512]{0,1:T(8,128)(2,1)S(1)}, u32[]{:S(2)}) copy-start(bf16[1536,512]{0,1:T(8,128)(2,1)S(1)} %get-tuple-element.107) | copy-start | bytes 4718596
  245.8 5.7 copy-start.52
  255.8 6.5 copy-start
  255.8 6.8 copy-start.43
  262.3 9.5 copy-start.54
  262.6 9.2 copy-start.38
  272.0 8.6 copy-start.34
  280.6 267.6 %all-gather.23.cloned.1.call-start = ((), (), s32[]{:S(2)}) async-start(), calls=%async_computation.17 | async-start | bytes 9437184 | tf_op jit(solution)/shard_map/all_gather | solution.py:107
  281.3 384.3 %all-gather.21.cloned.1.call-start = ((), (), s32[]{:S(2)}) async-start(), calls=%async_computation.16 | async-start | bytes 7864320 | tf_op jit(solution)/shard_map/all_gather | solution.py:152
  281.4 213.3 %copy-start.41 = (f32[2048]{0:T(1024)}, f32[2048]{0:T(1024)S(1)}, u32[]{:S(2)}) copy-start(f32[2048]{0:T(1024)S(1)} %convert_element_type.192) | copy-start | bytes 24580
  497.4 283.4 %all-gather.27.cloned.1.call-start = ((), (), s32[]{:S(2)}) async-start(), calls=%async_computation.20 | async-start | bytes 7864320 | tf_op jit(solution)/shard_map/all_gather | solution.py:167
  498.1 338.5 %all-gather.25.cloned.1.call-start = ((), (), s32[]{:S(2)}) async-start(), calls=%async_computation.18 | async-start | bytes 9437184 | tf_op jit(solution)/shard_map/all_gather | solution.py:108
  498.7 619.5 %reduce-scatter.15.cloned.1.call-start = ((), (), s32[]{:S(2)}) async-start(), calls=%async_computation.21 | async-start | bytes 15728640 | tf_op jit(solution)/shard_map/reduce_scatter | solution.py:173
  906.1 326.1 %reduce-scatter.13.cloned.1.call-start = ((), (), s32[]{:S(2)}) async-start(), calls=%async_computation.19 | async-start | bytes 7864320 | tf_op jit(solution)/shard_map/reduce_scatter | solution.py:158
  937.1 181.0 %copy-start.3 = (f32[384,2048]{1,0:T(8,128)S(1)}, f32[384,2048]{1,0:T(8,128)}, u32[]{:S(2)}) copy-start(f32[384,2048]{1,0:T(8,128)} %copy-done.2) | copy-start | bytes 9437188
  937.1 181.0 %copy-start.42 = (f32[2048]{0:T(1024)S(1)}, f32[2048]{0:T(1024)}, u32[]{:S(2)}) copy-start(f32[2048]{0:T(1024)} %copy-done.41) | copy-start | bytes 24580
  937.1 181.0 %copy-start.51 = (f32[384]{0:T(512)S(1)}, f32[384]{0:T(512)}, u32[]{:S(2)}) copy-start(f32[384]{0:T(512)} %copy-done.50) | copy-start | bytes 4612
  937.1 181.0 %copy-start.62 = (f32[384]{0:T(512)S(1)}, f32[384]{0:T(512)}, u32[]{:S(2)}) copy-start(f32[384]{0:T(512)} %copy-done.61) | copy-start | bytes 4612
  937.2 184.5 %copy-start.68 = (f32[384]{0:T(512)S(1)}, f32[384]{0:T(512)}, u32[]{:S(2)}) copy-start(f32[384]{0:T(512)} %copy-done.67) | copy-start | bytes 4612
  937.2 419.7 %all-gather.29.cloned.1.call-start = ((), (), s32[]{:S(2)}) async-start(), calls=%async_computation.22 | async-start | bytes 7864320 | tf_op jit(solution)/shard_map/all_gather | solution.py:181
  1232.1 6.5 copy-start.18
  1240.9 261.4 %reduce-scatter.29.cloned.1.call-start = ((), (), s32[]{:S(2)}) async-start(), calls=%async_computation.29 | async-start | bytes 9437184 | tf_op jit(solution)/shard_map/reduce_scatter | solution.py:241
  1260.4 244.7 %reduce-scatter.27.cloned.1.call-start = ((), (), s32[]{:S(2)}) async-start(), calls=%async_computation.28 | async-start | bytes 9437184 | tf_op jit(solution)/shard_map/reduce_scatter | solution.py:238
  1280.0 268.9 %reduce-scatter.25.cloned.1.call-start = ((), (), s32[]{:S(2)}) async-start(), calls=%async_computation.27 | async-start | bytes 2359296 | tf_op jit(solution)/shard_map/reduce_scatter | solution.py:235
  1280.7 84.0 %copy-start.14 = (pred[768,768]{0,1:T(8,128)(4,1)S(1)}, pred[768,768]{0,1:T(8,128)(4,1)}, u32[]{:S(2)}) copy-start(pred[768,768]{0,1:T(8,128)(4,1)} %copy-done.13) | copy-start | bytes 1769476
  1280.7 84.0 %copy-start.31 = (bf16[768,512]{0,1:T(8,128)(2,1)S(1)}, bf16[768,512]{0,1:T(8,128)(2,1)}, u32[]{:S(2)}) copy-start(bf16[768,512]{0,1:T(8,128)(2,1)} %copy-done.30) | copy-start | bytes 2359300
  1364.7 9.7 copy-start.32
  1374.4 10.9 copy-start.21
  1409.3 14.8 copy-start.22
  1409.3 14.8 copy-start.27
  1424.1 6.7 slice-start
  1424.1 6.7 slice-start.1
  1442.6 14.7 copy-start.23
  1442.6 14.7 copy-start.26
  1457.2 136.0 %reduce-scatter.21.cloned.1.call-start = ((), (), s32[]{:S(2)}) async-start(), calls=%async_computation.25 | async-start | bytes 2359296 | tf_op jit(solution)/shard_map/reduce_scatter | solution.py:229
  1457.4 17.1 copy-start.36
  1476.8 160.7 %reduce-scatter.23.cloned.1.call-start = ((), (), s32[]{:S(2)}) async-start(), calls=%async_computation.26 | async-start | bytes 2359296 | tf_op jit(solution)/shard_map/reduce_scatter | solution.py:232
  1477.4 204.5 %reduce-scatter.19.cloned.1.call-start = ((), (), s32[]{:S(2)}) async-start(), calls=%async_computation.24 | async-start | bytes 2359296 | tf_op jit(solution)/shard_map/reduce_scatter | solution.py:226
  1481.7 313.2 %reduce-scatter.17.cloned.1.call-start = ((), (), s32[]{:S(2)}) async-start(), calls=%async_computation.23 | async-start | bytes 7864320 | tf_op jit(solution)/shard_map/reduce_scatter | solution.py:214
  1481.7 12.2 copy-start.37
  1481.7 12.2 copy-start.77
  1502.3 6.0 copy-start.69
  1505.0 289.9 %copy-start.5 = (bf16[384,2048]{1,0:T(8,128)(2,1)S(1)}, bf16[384,2048]{1,0:T(8,128)(2,1)}, u32[]{:S(2)}) copy-start(bf16[384,2048]{1,0:T(8,128)(2,1)} %param.30) | copy-start | bytes 4718596
  1505.0 289.9 %copy-start.40 = (f32[2048]{0:T(1024)S(1)}, f32[2048]{0:T(1024)}, u32[]{:S(2)}) copy-start(f32[2048]{0:T(1024)} %copy-done.39) | copy-start | bytes 24580
  1505.0 289.9 %copy-start.49 = (f32[384]{0:T(512)S(1)}, f32[384]{0:T(512)}, u32[]{:S(2)}) copy-start(f32[384]{0:T(512)} %copy-done.48) | copy-start | bytes 4612
  1508.0 289.5 %copy-start.66 = (f32[384]{0:T(512)S(1)}, f32[384]{0:T(512)}, u32[]{:S(2)}) copy-start(f32[384]{0:T(512)} %copy-done.65) | copy-start | bytes 4612
  1508.0 289.5 %copy-start.57 = (f32[384]{0:T(512)S(1)}, f32[384]{0:T(512)}, u32[]{:S(2)}) copy-start(f32[384]{0:T(512)} %copy-done.56) | copy-start | bytes 4612
  1532.8 267.6 %copy-start.19 = (bf16[384,2048]{1,0:T(8,128)(2,1)S(1)}, bf16[384,2048]{1,0:T(8,128)(2,1)}, u32[]{:S(2)}) copy-start(bf16[384,2048]{1,0:T(8,128)(2,1)} %param.32) | copy-start | bytes 4718596
  1532.8 267.6 %copy-start.64 = (f32[384]{0:T(512)S(1)}, f32[384]{0:T(512)}, u32[]{:S(2)}) copy-start(f32[384]{0:T(512)} %copy-done.63) | copy-start | bytes 4612
  1794.9 5.5 copy-start.17
  (38 other events, 97.2 us)
Sparse Core Ops, SparseCore 0:
  9.9 30.5 all-gather.12
  42.4 27.7 all-gather.14
  72.1 27.7 all-gather.16
  101.9 115.3 all-gather.10
  219.0 26.2 all-gather.18
  280.7 210.2 reduce-scatter.10
  492.8 55.2 all-gather.22
  550.3 115.3 all-gather.20
  667.3 113.4 all-gather.26
  782.5 54.0 all-gather.24
  906.2 211.8 reduce-scatter.14
  1120.3 111.7 reduce-scatter.12
  1241.0 115.8 all-gather.28
  1360.2 69.4 reduce-scatter.28
  1433.0 71.5 reduce-scatter.26
  1507.7 41.1 reduce-scatter.24
  1552.0 41.1 reduce-scatter.20
  1596.3 41.1 reduce-scatter.22
  1640.8 41.1 reduce-scatter.18
  1684.1 110.7 reduce-scatter.16
where the time goes:
time: 1860 us; the launch traced here: 1850 us
  waiting for transfers between devices  1350 us (73%)
  matrix products  296 us (16%)
  other arithmetic  97.5 us (5%)
  blocking collectives  66.5 us (4%)
  local copies, waits for them, and re-layouts  22.7 us (1%)
    reduce_scatter x1, waiting for transfers between devices, on_device(): lax.psum_scatter(row_dot(attended, full_out), 'tensor', scatter_dimension...  210 us
    reduce_scatter x1, waiting for transfers between devices, on_device(): lax.psum_scatter(back_dot(grad_pre, full_up), 'tensor', scatter_dimension...  180 us
    all_gather x1, waiting for transfers between devices, on_device(): h_two_full = lax.all_gather(h_two, 'tensor', axis=0, tiled=True)  118 us
    all_gather x1, waiting for transfers between devices, on_device(): h_one_full = lax.all_gather(h_one, 'tensor', axis=0, tiled=True)  117 us
    reduce_scatter x1, waiting for transfers between devices, on_device(): lax.psum_scatter((back_dot(grad_qkv[:, :head_cols], full_query) * score_s...  111 us
    reduce_scatter x1, waiting for transfers between devices, on_device(): lax.psum_scatter(row_dot(act_low, full_down).astype(jnp.bfloat16), 'tenso...  110 us
    all_gather x1, waiting for transfers between devices, on_device(): grad_y_full = lax.all_gather(cotangent, 'tensor', axis=0, tiled=True)  96 us
    dot_general x5, matrix products, back_dot(): lax.dot_general(left_side, right_side, (((1,), (1,)), ((), ())), preferre...  94.2 us
  transfers between devices with their start and end apart: 20, of which 17 were waited for; matrix products, arithmetic and copies ran while one was open for 17% of the time, Pallas kernels for 0%

commit v1 on v0

--- a/solution.py
+++ b/solution.py
@@ -164,7 +164,23 @@
         + b_down.astype(jnp.float32)
     ).astype(jnp.bfloat16)
     grad_y = cotangent.astype(jnp.float32)
-    grad_y_full = lax.all_gather(cotangent, "tensor", axis=0, tiled=True)
+    value_now, arr_next, all_rows = (
+        lax.axis_size("tensor"),
+        lax.axis_index("tensor"),
+        cotangent.shape[0],
+    )
+    grad_y_full = jnp.zeros(
+        (*cotangent.shape[:0], value_now * all_rows, *cotangent.shape[0 + 1 :]), cotangent.dtype
+    )
+    response = cotangent
+    panels = tuple(((p, (p + 1) % value_now) for p in range(value_now)))
+    for hop_no in range(value_now):
+        y_new = (arr_next - hop_no) % value_now
+        grad_y_full = lax.dynamic_update_slice_in_dim(
+            grad_y_full, response, y_new * all_rows, axis=0
+        )
+        if hop_no < value_now - 1:
+            response = lax.ppermute(response, "tensor", panels)
     grad_down = left_dot(act_low, grad_y_full)
     grad_act = back_dot(grad_y_full, full_down)
     grad_pre = gelu_back(grad_act)[0].astype(jnp.bfloat16)

time: 1860 us -> 1780 us (0.957)
  waiting for transfers between devices: 1350 us -> 1260 us
    ppermute x0 -> x3, waiting for transfers between devices: none -> 141 us  [on_device(): response = lax.ppermute(response, 'tensor', panels)]
    all_gather x1 -> x0, waiting for transfers between devices: 96 us -> none  [on_device(): grad_y_full = lax.all_gather(cotangent, 'tensor', axis=0, tiled=True)]
    all_gather x1, waiting for transfers between devices: 118 us -> 44.8 us  [on_device(): h_two_full = lax.all_gather(h_two, 'tensor', axis=0, tiled=True)]
    all_gather x1, waiting for transfers between devices: 49.4 us -> 0.01 us  [on_device(): lax.all_gather(w_up, 'dp', axis=0, tiled=True)]
    all_gather x1, waiting for transfers between devices: 55.8 us -> 36.8 us  [on_device(): lax.all_gather(w_down, 'dp', axis=1, tiled=True)]
  transfers between devices with their start and end apart: 20 -> 22, of which waited for: 17 -> 19; matrix products, arithmetic and copies ran while one was open for 17% -> 18% of each run, Pallas kernels for 0% -> 0%
where the time goes in v1:
time: 1780 us; the launch traced here: 1770 us
  waiting for transfers between devices  1260 us (71%)
  matrix products  292 us (16%)
  other arithmetic  100 us (6%)
  blocking collectives  65.2 us (4%)
  local copies, waits for them, and re-layouts  30.5 us (2%)
    reduce_scatter x1, waiting for transfers between devices, on_device(): lax.psum_scatter(row_dot(attended, full_out), 'tensor', scatter_dimension...  210 us
    reduce_scatter x1, waiting for transfers between devices, on_device(): lax.psum_scatter(back_dot(grad_pre, full_up), 'tensor', scatter_dimension...  180 us
    ppermute x3, waiting for transfers between devices, on_device(): response = lax.ppermute(response, 'tensor', panels)  141 us
    all_gather x1, waiting for transfers between devices, on_device(): h_one_full = lax.all_gather(h_one, 'tensor', axis=0, tiled=True)  117 us
    reduce_scatter x1, waiting for transfers between devices, on_device(): lax.psum_scatter((back_dot(grad_qkv[:, :head_cols], full_query) * score_s...  111 us
    reduce_scatter x1, waiting for transfers between devices, on_device(): lax.psum_scatter(row_dot(act_low, full_down).astype(jnp.bfloat16), 'tenso...  111 us
    dot_general x5, matrix products, back_dot(): lax.dot_general(left_side, right_side, (((1,), (1,)), ((), ())), preferre...  92.1 us
    all_gather x1, waiting for transfers between devices, on_device(): grad_mix_full = lax.all_gather(grad_mix, 'tensor', axis=0, tiled=True)  76.2 us
  transfers between devices with their start and end apart: 22, of which 19 were waited for; matrix products, arithmetic and copies ran while one was open for 18% of the time, Pallas kernels for 0%

profile of v1, /device:TPU:0, one launch (start us, length us, event | category | flops | bytes accessed | tf_op | source)
XLA Modules:
  0.0 1773.2 jit_solution(13464957446907993665)
XLA Ops:
  15.7 3.2 fusion.54
  22.3 18.1 %all-gather.12.cloned.1.call-done = bf16[2048,512]{1,0:T(8,128)(2,1)} async-done(((bf16[256,512]{1,0:T(8,128)(2,1)}), bf16[2048,512]{1,0:T(8,128)(2,1)}) %all-gather.12.cloned.1.call-update) | async-done | bytes 2097168 | tf_op jit(solution)/shard_map/all_gather | solution.py:103
  40.5 29.7 %all-gather.14.cloned.1.call-done = bf16[2048,512]{1,0:T(8,128)(2,1)} async-done(((bf16[256,512]{1,0:T(8,128)(2,1)}), bf16[2048,512]{1,0:T(8,128)(2,1)}) %all-gather.14.cloned.1.call-update) | async-done | bytes 2097168 | tf_op jit(solution)/shard_map/all_gather | solution.py:104
  70.1 29.7 %all-gather.16.cloned.1.call-done = bf16[2048,512]{1,0:T(8,128)(2,1)} async-done(((bf16[256,512]{1,0:T(8,128)(2,1)}), bf16[2048,512]{1,0:T(8,128)(2,1)}) %all-gather.16.cloned.1.call-update) | async-done | bytes 2097168 | tf_op jit(solution)/shard_map/all_gather | solution.py:105
  99.8 117.4 %all-gather.10.cloned.1.call-done = bf16[1536,2048]{1,0:T(8,128)(2,1)} async-done(((bf16[384,2048]{1,0:T(8,128)(2,1)}), bf16[1536,2048]{1,0:T(8,128)(2,1)}) %all-gather.10.cloned.1.call-update) | async-done | bytes 6291472 | tf_op jit(solution)/shard_map/all_gather | solution.py:119
  217.2 17.0 fusion.99
  237.2 3.9 fusion.60
  244.8 3.1 fusion.80
  247.9 3.1 select_reduce_fusion
  251.1 5.1 fusion
  257.9 9.1 fusion.79
  267.2 8.5 fusion.101
  276.6 209.5 %reduce-scatter.11.cloned.1.call-done = f32[384,2048]{1,0:T(8,128)} async-done(((f32[1536,2048]{1,0:T(8,128)}), f32[384,2048]{1,0:T(8,128)}) %reduce-scatter.11.cloned.1.call-update) | async-done | bytes 3145744 | tf_op jit(solution)/shard_map/reduce_scatter | solution.py:145
  494.9 36.4 %collective-permute-done = bf16[384,2048]{1,0:T(8,128)(2,1)S(1)} collective-permute-done((bf16[384,2048]{1,0:T(8,128)(2,1)S(1)}, bf16[384,2048]{1,0:T(8,128)(2,1)S(1)}, u32[]{:S(2)}, u32[]{:S(2)}) %collective-permute-start) | collective-permute-done | bytes 1572896 | tf_op jit(solution)/shard_map/ppermute | solution.py:183
  531.3 48.6 %collective-permute-done.1 = bf16[384,2048]{1,0:T(8,128)(2,1)} collective-permute-done((bf16[384,2048]{1,0:T(8,128)(2,1)S(1)}, bf16[384,2048]{1,0:T(8,128)(2,1)}, u32[]{:S(2)}, u32[]{:S(2)}) %collective-permute-start.1) | collective-permute-done | bytes 1572896 | tf_op jit(solution)/shard_map/ppermute | solution.py:183
  579.8 11.5 collective-permute-start.2
  591.3 3.5 broadcast_in_dim.50
  597.3 2.7 constant_dynamic-update-slice_fusion.1
  600.1 56.1 %collective-permute-done.2 = bf16[384,2048]{1,0:T(8,128)(2,1)} collective-permute-done((bf16[384,2048]{1,0:T(8,128)(2,1)}, bf16[384,2048]{1,0:T(8,128)(2,1)}, u32[]{:S(2)}, u32[]{:S(2)}) %collective-permute-start.2) | collective-permute-done | bytes 1572896 | tf_op jit(solution)/shard_map/ppermute | solution.py:183
  656.2 2.7 constant_dynamic-update-slice_fusion
  658.9 44.8 %all-gather.20.cloned.1.call-done = bf16[1536,2048]{1,0:T(8,128)(2,1)} async-done(((bf16[384,2048]{1,0:T(8,128)(2,1)}), bf16[1536,2048]{1,0:T(8,128)(2,1)}) %all-gather.20.cloned.1.call-update) | async-done | bytes 6291472 | tf_op jit(solution)/shard_map/all_gather | solution.py:152
  703.8 19.1 %fusion.102 = f32[1536,2048]{1,0:T(8,128)} fusion(bf16[1536,2048]{1,0:T(8,128)(2,1)} %all-gather.20.cloned.1.call-done, bf16[2048,2048]{1,0:T(8,128)(2,1)} %all-gather.22.cloned.1.call-done), kind=kOutput, calls=%fused_computation.167 | convolution fusion | flops 12884901888 | bytes 27262976 | tf_op jit(solution)/shard_map/dot_general | solution.py:25
  722.9 36.8 %all-gather.24.cloned.1.call-done = bf16[2048,2048]{1,0:T(8,128)(2,1)} async-done(((bf16[2048,256]{1,0:T(8,128)(2,1)}), bf16[2048,2048]{1,0:T(8,128)(2,1)}) %all-gather.24.cloned.1.call-update) | async-done | bytes 8388624 | tf_op jit(solution)/shard_map/all_gather | solution.py:108
  759.7 48.6 %convert_reduce_fusion = (f32[2048]{0:T(1024)}, bf16[1536,2048]{1,0:T(8,128)(2,1)S(1)}, f32[1536,2048]{1,0:T(8,128)}) fusion(f32[1536,2048]{1,0:T(8,128)} %fusion.102, f32[2048]{0:T(1024)S(1)} %convert_element_type.195, bf16[1536,2048]{1,0:T(8,128)(2,1)} %constant_dynamic-update-slice_fusion, bf16[2048,2048]{1,0:T(8,128)(2,1)} %all-gather.24.cloned.1.call-done), kind=kOutput, calls=%fused_computation.9 | convolution fusion | flops 13120829440 | bytes 46153728 | tf_op jit(solution)/shard_map/dot_general | solution.py:35
  808.3 2.6 copy-done.80
  810.9 16.1 fusion.103
  827.1 10.7 multiply_convert_fusion.1
  837.9 2.7 copy-done.29
  840.6 17.5 convolution_convert_fusion.2
  858.8 180.4 %reduce-scatter.15.cloned.1.call-done = f32[384,2048]{1,0:T(8,128)} async-done(((f32[1536,2048]{1,0:T(8,128)}), f32[384,2048]{1,0:T(8,128)}) %reduce-scatter.15.cloned.1.call-update) | async-done | bytes 3145744 | tf_op jit(solution)/shard_map/reduce_scatter | solution.py:189
  1039.2 3.5 multiply_reduce_fusion.2
  1042.7 110.6 %reduce-scatter.13.cloned.1.call-done = bf16[384,2048]{1,0:T(8,128)(2,1)} async-done(((bf16[1536,2048]{1,0:T(8,128)(2,1)}), bf16[384,2048]{1,0:T(8,128)(2,1)}) %reduce-scatter.13.cloned.1.call-update) | async-done | bytes 1572880 | tf_op jit(solution)/shard_map/reduce_scatter | solution.py:158
  1153.3 4.8 fusion.92
  1162.1 19.4 %convolution_convert_fusion = bf16[2048,2048]{1,0:T(8,128)(2,1)} fusion(bf16[1536,2048]{1,0:T(8,128)(2,1)} %copy-done.29, bf16[1536,2048]{1,0:T(8,128)(2,1)} %constant_dynamic-update-slice_fusion), kind=kOutput, calls=%fused_computation.39 | convolution fusion | flops 12889096192 | bytes 20971520 | tf_op jit(solution)/shard_map/dot_general | solution.py:29
  1181.7 19.3 %convolution_convert_fusion.1 = bf16[2048,2048]{1,0:T(8,128)(2,1)} fusion(bf16[1536,2048]{1,0:T(8,128)(2,1)} %all-gather.20.cloned.1.call-done, bf16[1536,2048]{1,0:T(8,128)(2,1)} %copy-done.80), kind=kOutput, calls=%fused_computation.40 | convolution fusion | flops 12889096192 | bytes 20971520 | tf_op jit(solution)/shard_map/dot_general | solution.py:29
  1201.8 76.2 %all-gather.26.cloned.1.call-done = bf16[1536,2048]{1,0:T(8,128)(2,1)} async-done(((bf16[384,2048]{1,0:T(8,128)(2,1)}), bf16[1536,2048]{1,0:T(8,128)(2,1)}) %all-gather.26.cloned.1.call-update) | async-done | bytes 6291472 | tf_op jit(solution)/shard_map/all_gather | solution.py:197
  1278.0 6.9 convolution_convert_fusion.4
  1285.9 9.6 multiply_reduce_fusion.1
  1295.5 10.9 multiply_convert_fusion.2
  1306.4 4.4 fusion.77
  1310.8 2.8 convolution_bitcast_fusion.1
  1313.6 17.0 multiply_reduce_fusion
  1330.6 14.8 multiply_convert_fusion
  1345.4 2.6 fusion.68
  1348.0 4.1 fusion.78
  1352.1 4.4 fusion.72
  1356.5 7.4 convolution_convert_fusion.3
  1364.0 12.9 convert_reduce_fusion.5
  1377.1 17.0 fusion.100
  1397.1 4.2 fusion.39
  1401.4 12.2 fusion.40
  1413.6 8.2 add_convert_fusion
  1421.9 2.8 convert_element_type.233
  1425.8 2.8 convert_element_type.230
  1430.4 23.2 %all-reduce.3 = (f32[512]{0:T(512)}, f32[512]{0:T(512)}, f32[2048]{0:T(1024)}) all-reduce(f32[512]{0:T(512)S(1)} %multiply_bitcast_fusion, f32[512]{0:T(512)S(1)} %bitcast.105, f32[2048]{0:T(1024)S(1)} %copy-done.70), channel_id=1, replica_groups=mesh['dp'=8,'tensor'=4] {'dp'}, use_global_device_ids=true, to_apply=%region_24.25 | all-reduce | flops 3072 | bytes 24576 | tf_op jit(solution)/shard_map/psum | solution.py:261
  1453.6 16.5 reduce-scatter.25.cloned.1.call-done
  1471.9 42.5 %reduce-scatter.21.cloned.1.call-done = bf16[256,512]{1,0:T(8,128)(2,1)} async-done(((bf16[2048,512]{1,0:T(8,128)(2,1)}), bf16[256,512]{1,0:T(8,128)(2,1)}) %reduce-scatter.21.cloned.1.call-update) | async-done | bytes 262160 | tf_op jit(solution)/shard_map/reduce_scatter | solution.py:245
  1516.2 42.5 %reduce-scatter.23.cloned.1.call-done = bf16[256,512]{1,0:T(8,128)(2,1)} async-done(((bf16[2048,512]{1,0:T(8,128)(2,1)}), bf16[256,512]{1,0:T(8,128)(2,1)}) %reduce-scatter.23.cloned.1.call-update) | async-done | bytes 262160 | tf_op jit(solution)/shard_map/reduce_scatter | solution.py:248
  1560.5 42.5 %reduce-scatter.19.cloned.1.call-done = bf16[256,512]{1,0:T(8,128)(2,1)} async-done(((bf16[2048,512]{1,0:T(8,128)(2,1)}), bf16[256,512]{1,0:T(8,128)(2,1)}) %reduce-scatter.19.cloned.1.call-update) | async-done | bytes 262160 | tf_op jit(solution)/shard_map/reduce_scatter | solution.py:242
  1604.8 111.3 %reduce-scatter.17.cloned.1.call-done = bf16[384,2048]{1,0:T(8,128)(2,1)} async-done(((bf16[1536,2048]{1,0:T(8,128)(2,1)}), bf16[384,2048]{1,0:T(8,128)(2,1)}) %reduce-scatter.17.cloned.1.call-update) | async-done | bytes 1572880 | tf_op jit(solution)/shard_map/reduce_scatter | solution.py:230
  1716.1 2.5 convert_reduce_fusion.1
  1718.7 2.9 fusion.58
  1721.7 2.8 convert_reduce_fusion.3
  1724.5 42.0 %all-reduce.2 = (f32[2048]{0:T(1024)}, f32[2048]{0:T(1024)}, f32[2048]{0:T(1024)}, f32[2048]{0:T(1024)}, f32[2048]{0:T(1024)}, /*index=5*/f32[2048]{0:T(1024)}) all-reduce(f32[2048]{0:T(1024)S(1)} %get-tuple-element.83, f32[2048]{0:T(1024)S(1)} %get-tuple-element.86, ...), channel_id=1, replica_groups=mesh['dp'=8,'tensor'=4] {'dp','tensor'}, use_global_device_ids=true, to_apply=%region_19.20 | all-reduce | flops 12288 | bytes 98304 | tf_op jit(solution)/shard_map/psum | solution.py:265
  (259 shorter events, 52.3 us)
Async XLA Ops:
  7.2 12.4 copy-start.48
  7.2 12.4 copy-start.76
  7.2 12.5 copy-start.77
  7.2 33.2 %all-gather.12.cloned.1.call-start = ((), (), s32[]{:S(2)}) async-start(), calls=%async_computation.11 | async-start | bytes 2359296 | tf_op jit(solution)/shard_map/all_gather | solution.py:103
  8.0 62.2 %all-gather.14.cloned.1.call-start = ((), (), s32[]{:S(2)}) async-start(), calls=%async_computation.12 | async-start | bytes 2359296 | tf_op jit(solution)/shard_map/all_gather | solution.py:104
  8.7 91.1 %all-gather.16.cloned.1.call-start = ((), (), s32[]{:S(2)}) async-start(), calls=%async_computation.13 | async-start | bytes 2359296 | tf_op jit(solution)/shard_map/all_gather | solution.py:105
  9.4 207.8 %all-gather.10.cloned.1.call-start = ((), (), s32[]{:S(2)}) async-start(), calls=%async_computation.10 | async-start | bytes 7864320 | tf_op jit(solution)/shard_map/all_gather | solution.py:119
  19.0 248.2 %all-gather.18.cloned.1.call-start = ((), (), s32[]{:S(2)}) async-start(), calls=%async_computation.14 | async-start | bytes 2359296 | tf_op jit(solution)/shard_map/all_gather | solution.py:106
  19.5 466.6 %reduce-scatter.11.cloned.1.call-start = ((), (), s32[]{:S(2)}) async-start(), calls=%async_computation.15 | async-start | bytes 15728640 | tf_op jit(solution)/shard_map/reduce_scatter | solution.py:145
  20.1 224.7 %copy-start.13 = (pred[768,768]{0,1:T(8,128)(4,1)}, pred[768,768]{0,1:T(8,128)(4,1)S(1)}, u32[]{:S(2)}) copy-start(pred[768,768]{0,1:T(8,128)(4,1)S(1)} %fusion.69) | copy-start | bytes 1769476
  22.3 235.2 %copy-start.6 = (pred[768,1536]{1,0:T(8,128)(4,1)}, pred[768,1536]{1,0:T(8,128)(4,1)S(1)}, u32[]{:S(2)}) copy-start(pred[768,1536]{1,0:T(8,128)(4,1)S(1)} %fusion.36) | copy-start | bytes 3538948
  237.2 10.7 copy-start.11
  241.1 16.4 copy-start.15
  251.1 6.8 copy-start.44
  257.5 9.5 copy-start.55
  267.1 8.6 copy-start.36
  275.7 210.4 %copy-start.4 = (bf16[384,2048]{1,0:T(8,128)(2,1)S(1)}, bf16[384,2048]{1,0:T(8,128)(2,1)}, u32[]{:S(2)}) copy-start(bf16[384,2048]{1,0:T(8,128)(2,1)} %param.30) | copy-start | bytes 4718596
  275.8 383.2 %all-gather.22.cloned.1.call-start = ((), (), s32[]{:S(2)}) async-start(), calls=%async_computation.17 | async-start | bytes 9437184 | tf_op jit(solution)/shard_map/all_gather | solution.py:107
  276.5 427.3 %all-gather.20.cloned.1.call-start = ((), (), s32[]{:S(2)}) async-start(), calls=%async_computation.16 | async-start | bytes 7864320 | tf_op jit(solution)/shard_map/all_gather | solution.py:152
  276.6 215.9 %copy-start.42 = (f32[2048]{0:T(1024)}, f32[2048]{0:T(1024)S(1)}, u32[]{:S(2)}) copy-start(f32[2048]{0:T(1024)S(1)} %convert_element_type.192) | copy-start | bytes 24580
  488.5 102.8 %copy-start.74 = (bf16[2048]{0:T(1024)(128)(2,1)S(1)}, bf16[2048]{0:T(1024)(128)(2,1)}, u32[]{:S(2)}) copy-start(bf16[2048]{0:T(1024)(128)(2,1)} %param.45) | copy-start | bytes 12292
  492.5 267.1 %all-gather.24.cloned.1.call-start = ((), (), s32[]{:S(2)}) async-start(), calls=%async_computation.18 | async-start | bytes 9437184 | tf_op jit(solution)/shard_map/all_gather | solution.py:108
  493.3 545.9 %reduce-scatter.15.cloned.1.call-start = ((), (), s32[]{:S(2)}) async-start(), calls=%async_computation.20 | async-start | bytes 15728640 | tf_op jit(solution)/shard_map/reduce_scatter | solution.py:189
  493.3 37.9 %collective-permute-start = (bf16[384,2048]{1,0:T(8,128)(2,1)S(1)}, bf16[384,2048]{1,0:T(8,128)(2,1)S(1)}, u32[]{:S(2)}, u32[]{:S(2)}) collective-permute-start(bf16[384,2048]{1,0:T(8,128)(2,1)S(1)} %copy-done.18), channel_id=1, source_target_pairs={{0,1},{1,2},{2,3},{3,0},{4,5},{5,6},{6,7},{7,4},{8,9},{9,10},{10,1... | collective-permute-start | bytes 4718600 | tf_op jit(solution)/shard_map/ppermute | solution.py:183
  531.3 48.6 %collective-permute-start.1 = (bf16[384,2048]{1,0:T(8,128)(2,1)S(1)}, bf16[384,2048]{1,0:T(8,128)(2,1)}, u32[]{:S(2)}, u32[]{:S(2)}) collective-permute-start(bf16[384,2048]{1,0:T(8,128)(2,1)S(1)} %collective-permute-done), channel_id=1, source_target_pairs={{0,1},{1,2},{2,3},{3,0},{4,5},{5,6},{6,7},{7,4},{8,9},{9,10},{10,1... | collective-permute-start | bytes 4718600 | tf_op jit(solution)/shard_map/ppermute | solution.py:183
  579.8 76.4 %collective-permute-start.2 = (bf16[384,2048]{1,0:T(8,128)(2,1)}, bf16[384,2048]{1,0:T(8,128)(2,1)}, u32[]{:S(2)}, u32[]{:S(2)}) collective-permute-start(bf16[384,2048]{1,0:T(8,128)(2,1)} %collective-permute-done.1), channel_id=1, source_target_pairs={{0,1},{1,2},{2,3},{3,0},{4,5},{5,6},{6,7},{7,4},{8,9},{9,10},{10,1... | collective-permute-start | bytes 4718600 | tf_op jit(solution)/shard_map/ppermute | solution.py:183
  759.7 51.3 %copy-start.78 = (bf16[2048,2048]{1,0:T(8,128)(2,1)S(1)}, bf16[2048,2048]{1,0:T(8,128)(2,1)}, u32[]{:S(2)}) copy-start(bf16[2048,2048]{1,0:T(8,128)(2,1)} %all-gather.22.cloned.1.call-done) | copy-start | bytes 25165828
  827.1 326.2 %reduce-scatter.13.cloned.1.call-start = ((), (), s32[]{:S(2)}) async-start(), calls=%async_computation.19 | async-start | bytes 7864320 | tf_op jit(solution)/shard_map/reduce_scatter | solution.py:158
  858.1 181.1 %copy-start.3 = (f32[384,2048]{1,0:T(8,128)S(1)}, f32[384,2048]{1,0:T(8,128)}, u32[]{:S(2)}) copy-start(f32[384,2048]{1,0:T(8,128)} %copy-done.2) | copy-start | bytes 9437188
  858.1 181.1 %copy-start.43 = (f32[2048]{0:T(1024)S(1)}, f32[2048]{0:T(1024)}, u32[]{:S(2)}) copy-start(f32[2048]{0:T(1024)} %copy-done.42) | copy-start | bytes 24580
  858.1 181.1 %copy-start.52 = (f32[384]{0:T(512)S(1)}, f32[384]{0:T(512)}, u32[]{:S(2)}) copy-start(f32[384]{0:T(512)} %copy-done.51) | copy-start | bytes 4612
  858.1 181.1 %copy-start.63 = (f32[384]{0:T(512)S(1)}, f32[384]{0:T(512)}, u32[]{:S(2)}) copy-start(f32[384]{0:T(512)} %copy-done.62) | copy-start | bytes 4612
  858.1 184.6 %copy-start.69 = (f32[384]{0:T(512)S(1)}, f32[384]{0:T(512)}, u32[]{:S(2)}) copy-start(f32[384]{0:T(512)} %copy-done.68) | copy-start | bytes 4612
  858.1 419.9 %all-gather.26.cloned.1.call-start = ((), (), s32[]{:S(2)}) async-start(), calls=%async_computation.21 | async-start | bytes 7864320 | tf_op jit(solution)/shard_map/all_gather | solution.py:197
  1162.0 259.9 %reduce-scatter.29.cloned.1.call-start = ((), (), s32[]{:S(2)}) async-start(), calls=%async_computation.28 | async-start | bytes 9437184 | tf_op jit(solution)/shard_map/reduce_scatter | solution.py:257
  1181.5 244.3 %reduce-scatter.27.cloned.1.call-start = ((), (), s32[]{:S(2)}) async-start(), calls=%async_computation.27 | async-start | bytes 9437184 | tf_op jit(solution)/shard_map/reduce_scatter | solution.py:254
  1201.1 269.0 %reduce-scatter.25.cloned.1.call-start = ((), (), s32[]{:S(2)}) async-start(), calls=%async_computation.26 | async-start | bytes 2359296 | tf_op jit(solution)/shard_map/reduce_scatter | solution.py:251
  1201.8 84.1 %copy-start.14 = (pred[768,768]{0,1:T(8,128)(4,1)S(1)}, pred[768,768]{0,1:T(8,128)(4,1)}, u32[]{:S(2)}) copy-start(pred[768,768]{0,1:T(8,128)(4,1)} %copy-done.13) | copy-start | bytes 1769476
  1201.8 84.0 %copy-start.33 = (bf16[768,512]{0,1:T(8,128)(2,1)S(1)}, bf16[768,512]{0,1:T(8,128)(2,1)}, u32[]{:S(2)}) copy-start(bf16[768,512]{0,1:T(8,128)(2,1)} %copy-done.32) | copy-start | bytes 2359300
  1285.9 9.6 copy-start.34
  1306.3 7.2 copy-start.7
  1306.3 7.2 copy-start.16
  1306.3 7.2 copy-start.30
  1330.6 14.8 copy-start.23
  1330.6 14.8 copy-start.28
  1345.4 6.7 slice-start
  1356.5 7.5 copy-start.31
  1364.0 13.0 copy-start.24
  1364.0 13.0 copy-start.27
  1376.9 137.5 %reduce-scatter.21.cloned.1.call-start = ((), (), s32[]{:S(2)}) async-start(), calls=%async_computation.24 | async-start | bytes 2359296 | tf_op jit(solution)/shard_map/reduce_scatter | solution.py:245
  1377.1 17.0 copy-start.38
  1396.5 162.2 %reduce-scatter.23.cloned.1.call-start = ((), (), s32[]{:S(2)}) async-start(), calls=%async_computation.25 | async-start | bytes 2359296 | tf_op jit(solution)/shard_map/reduce_scatter | solution.py:248
  1397.0 205.9 %reduce-scatter.19.cloned.1.call-start = ((), (), s32[]{:S(2)}) async-start(), calls=%async_computation.23 | async-start | bytes 2359296 | tf_op jit(solution)/shard_map/reduce_scatter | solution.py:242
  1401.3 12.3 copy-start.39
  1401.3 314.8 %reduce-scatter.17.cloned.1.call-start = ((), (), s32[]{:S(2)}) async-start(), calls=%async_computation.22 | async-start | bytes 7864320 | tf_op jit(solution)/shard_map/reduce_scatter | solution.py:230
  1401.4 12.2 copy-start.79
  1421.8 8.6 copy-start.70
  1421.8 294.3 %copy-start.5 = (bf16[384,2048]{1,0:T(8,128)(2,1)S(1)}, bf16[384,2048]{1,0:T(8,128)(2,1)}, u32[]{:S(2)}) copy-start(bf16[384,2048]{1,0:T(8,128)(2,1)} %param.30) | copy-start | bytes 4718596
  1421.9 294.3 %copy-start.41 = (f32[2048]{0:T(1024)S(1)}, f32[2048]{0:T(1024)}, u32[]{:S(2)}) copy-start(f32[2048]{0:T(1024)} %copy-done.40) | copy-start | bytes 24580
  1421.9 294.2 %copy-start.50 = (f32[384]{0:T(512)S(1)}, f32[384]{0:T(512)}, u32[]{:S(2)}) copy-start(f32[384]{0:T(512)} %copy-done.49) | copy-start | bytes 4612
  1424.7 293.9 %copy-start.67 = (f32[384]{0:T(512)S(1)}, f32[384]{0:T(512)}, u32[]{:S(2)}) copy-start(f32[384]{0:T(512)} %copy-done.66) | copy-start | bytes 4612
  1424.7 293.9 %copy-start.58 = (f32[384]{0:T(512)S(1)}, f32[384]{0:T(512)}, u32[]{:S(2)}) copy-start(f32[384]{0:T(512)} %copy-done.57) | copy-start | bytes 4612
  1428.6 293.0 %copy-start.20 = (bf16[384,2048]{1,0:T(8,128)(2,1)S(1)}, bf16[384,2048]{1,0:T(8,128)(2,1)}, u32[]{:S(2)}) copy-start(bf16[384,2048]{1,0:T(8,128)(2,1)} %param.32) | copy-start | bytes 4718596
  1428.6 293.0 %copy-start.65 = (f32[384]{0:T(512)S(1)}, f32[384]{0:T(512)}, u32[]{:S(2)}) copy-start(f32[384]{0:T(512)} %copy-done.64) | copy-start | bytes 4612
  (42 other events, 138.7 us)
Sparse Core Ops, SparseCore 0:
  9.9 30.4 all-gather.11
  42.3 27.7 all-gather.13
  72.0 27.7 all-gather.15
  101.8 115.3 all-gather.9
  218.9 26.2 all-gather.17
  275.9 210.2 reduce-scatter.10
  488.0 55.2 all-gather.21
  545.5 158.1 all-gather.19
  705.6 53.9 all-gather.23
  827.2 211.8 reduce-scatter.14
  1041.4 111.7 reduce-scatter.12
  1162.2 115.8 all-gather.25
  1281.5 69.4 reduce-scatter.28
  1354.3 71.4 reduce-scatter.26
  1428.9 41.1 reduce-scatter.24
  1473.3 41.0 reduce-scatter.20
  1517.5 41.1 reduce-scatter.22
  1561.8 41.1 reduce-scatter.18
  1605.3 110.7 reduce-scatter.16
